TPU v7x, 32 devices: a whole 2x2x4 slice. The times are simulated.
32 devices in a mesh: kpt: 2 (over x), gx: 16 (over z, y, core).
Axes of the slice: x: 2, y: 2, z: 4, core: 2. Of those that a mesh axis runs over, the one named last changes fastest.
Arguments:
- e_field: float32 [2, 3, 64, 512, 128], P(None, None, ('kpt', 'gx')), parts along dimension 2, may hold values from -6 to 6
- h_field: float32 [2, 3, 64, 512, 128], P(None, None, ('kpt', 'gx')), parts along dimension 2, may hold values from -6 to 6
- labels: int32 [64, 512, 128], P(('kpt', 'gx')), parts along dimension 0, may hold values from 0 to 3
- kpoint: int32 [4], P('kpt'), parts along dimension 0, may hold values from 0 to 15
- eps_inf: float32 [4], replicated, may hold values from 1 to 12
- delta_eps: float32 [4], replicated, may hold values from 0.5 to 4
- omega_zero: float32 [4], replicated, may hold values from 0.2 to 1
- damping: float32 [4], replicated, may hold values from 0.05 to 0.8
Outputs:
- e_final: float32 [2, 3, 64, 512, 128], P(None, None, ('kpt', 'gx')), parts along dimension 2
- h_final: float32 [2, 3, 64, 512, 128], P(None, None, ('kpt', 'gx')), parts along dimension 2
There are 2 independent parts, one for each index of `kpt`. A program takes and returns all parts, laid end to end along the dimension named above; an argument that names none is the same for every part. Nothing has to cross between parts.
Inputs may be any that keep to these rules, and one draw needn't show every extreme that they name: `kpoint`: entry 0 indexes the k-point along x, entry 1 along y, out of 16 each.
All inputs are finite; a program needn't handle non-finite values.
Results may differ from a plain program's by a relative error of at most 0.00002.
Values sent between devices are 32-bit elements; how exact they have to be, the bound alone decides.
A program may use at most 128 MiB of HBM per device.

v0:
```python
import math

import jax
import jax.numpy as jnp
from jax import lax
from jax.sharding import PartitionSpec as P

ITERS = 12
KGRID = 16


time_step = 0.5


def shifted(value, axis, by):
    size = lax.axis_size(axis)
    return lax.ppermute(value, axis, [(i, (i + by) % size) for i in range(size)])


def cmul(field, cosv, sinv):
    return jnp.stack([field[0] * cosv - field[1] * sinv, field[0] * sinv + field[1] * cosv])


def next_y(field, cosv, sinv):
    rolled = jnp.roll(field, -1, axis=-2)
    last = cmul(rolled[..., -1:, :], cosv, sinv)
    return jnp.concatenate([rolled[..., :-1, :], last], axis=-2)


def prev_y(field, cosv, sinv):
    rolled = jnp.roll(field, 1, axis=-2)
    first = cmul(rolled[..., :1, :], cosv, -sinv)
    return jnp.concatenate([first, rolled[..., 1:, :]], axis=-2)


def next_z(field):
    zeros = jnp.zeros(field.shape[:-1] + (1,), jnp.float32)
    return jnp.concatenate([field[..., 1:], zeros], axis=-1)


def prev_z(field):
    zeros = jnp.zeros(field.shape[:-1] + (1,), jnp.float32)
    return jnp.concatenate([zeros, field[..., :-1]], axis=-1)


def per_cell(labels, table):
    picked = jnp.zeros(labels.shape, jnp.float32)
    for label in range(table.shape[0]):
        picked = picked + jnp.where(labels == label, table[label], jnp.float32(0.0))
    return picked


def update_magnetic(efield, hfield, right_ey, right_ez, cos_y, sin_y):
    ex, ey, ez = (efield[:, 0], efield[:, 1], efield[:, 2])
    next_ey = jnp.concatenate([ey[:, 1:], right_ey], axis=1)
    next_ez = jnp.concatenate([ez[:, 1:], right_ez], axis=1)
    curl_x = next_y(ez, cos_y, sin_y) - ez - (next_z(ey) - ey)
    curl_y = next_z(ex) - ex - (next_ez - ez)
    curl_z = next_ey - ey - (next_y(ex, cos_y, sin_y) - ex)
    return hfield - time_step * jnp.stack([curl_x, curl_y, curl_z], axis=1)


def update_electric(efield, hfield, polar, current, left_hy, left_hz, coeffs, cos_y, sin_y):
    ce, ja, jb, de = coeffs
    hx, hy, hz = (hfield[:, 0], hfield[:, 1], hfield[:, 2])
    prev_hy = jnp.concatenate([left_hy, hy[:, :-1]], axis=1)
    prev_hz = jnp.concatenate([left_hz, hz[:, :-1]], axis=1)
    kurl_x = hz - prev_y(hz, cos_y, sin_y) - (hy - prev_z(hy))
    kurl_y = hx - prev_z(hx) - (hz - prev_hz)
    kurl_z = hy - prev_hy - (hx - prev_y(hx, cos_y, sin_y))
    kurl = jnp.stack([kurl_x, kurl_y, kurl_z], axis=1)
    current = ja * current + jb * (de * efield - polar)
    polar = polar + time_step * current
    efield = efield + ce * (kurl - current)
    return (efield, polar, current)


def shards(e_field, h_field, labels, kpoint, eps_inf, delta_eps, omega_zero, damping):
    theta_x = jnp.float32(2.0 * math.pi) * kpoint[0].astype(jnp.float32) / KGRID
    theta_y = jnp.float32(2.0 * math.pi) * kpoint[1].astype(jnp.float32) / KGRID
    cos_x, sin_x = (jnp.cos(theta_x), jnp.sin(theta_x))
    cos_y, sin_y = (jnp.cos(theta_y), jnp.sin(theta_y))
    half = damping * time_step / 2.0
    coeffs = (
        per_cell(labels, time_step / eps_inf),
        per_cell(labels, (1.0 - half) / (1.0 + half)),
        per_cell(labels, time_step * omega_zero * omega_zero / (1.0 + half)),
        per_cell(labels, delta_eps),
    )
    position = lax.axis_index("gx")
    at_first = position == 0
    at_last = position == lax.axis_size("gx") - 1
    start_ghost = jnp.zeros((2, 2, 1) + h_field.shape[3:], jnp.float32)

    def advance(step, carry):
        efield, hfield, polar, current, ghost = carry
        planes = efield[:, 1:3, 0:1]
        right = shifted(planes, "gx", -1)
        right = jnp.where(at_last, cmul(right, cos_x, sin_x), right)
        new_h = update_magnetic(efield, hfield, right[:, 0], right[:, 1], cos_y, sin_y)
        hplanes = new_h[:, 1:3, -1:]
        left = shifted(hplanes, "gx", 1)
        left = jnp.where(at_first, cmul(left, cos_x, -sin_x), left)
        left_hy, left_hz = (left[:, 0], left[:, 1])
        new_e, polar, current = update_electric(
            efield, new_h, polar, current, left_hy, left_hz, coeffs, cos_y, sin_y
        )
        return (new_e, new_h, polar, current, ghost)

    zeros = jnp.zeros(e_field.shape, jnp.float32)
    efield, hfield, polar, current, ghost = lax.fori_loop(
        0, ITERS, advance, (e_field, h_field, zeros, zeros, start_ghost)
    )
    return (efield, hfield)


def solution(mesh):
    placed = (
        P(None, None, ("kpt", "gx"), None, None),
        P(None, None, ("kpt", "gx"), None, None),
        P(("kpt", "gx"), None, None),
        P("kpt"),
        P(),
        P(),
        P(),
        P(),
    )
    return jax.shard_map(
        shards,
        mesh=mesh,
        in_specs=placed,
        out_specs=(
            P(None, None, ("kpt", "gx"), None, None),
            P(None, None, ("kpt", "gx"), None, None),
        ),
        check_vma=False,
    )
```

profile of v0, /device:TPU:1, one launch (start us, length us, event | category | flops | bytes accessed | tf_op | source)
XLA Modules:
  0.0 529.8 jit_solution(3203353989150114886)
XLA Ops:
  0.6 3.8 copy.112
  9.2 4.9 select_add_fusion
  14.0 9.1 %select_add_fusion.1 = (f32[2,512,128]{2,1,0:T(8,128)}, f32[2,512,128]{2,1,0:T(8,128)}, f32[2,512,128]{2,1,0:T(8,128)}) fusion(pred[2,512,128]{2,1,0:T(8,128)(4,1)S(1)} %get-tuple-element.245, pred[2,512,128]{2,1,0:T(8,128)(4,1)S(1)} %get-tuple-element.244, pred[2,512,128]{2,1,0:T(8,128)(4,1)S(1)} %get-tuple-element.243, ...), kind=kLoop, calls=%fused_computation.64 | loop fusion | flops 2752512 | bytes 2097200 | tf_op jit(solution)/shard_map/add | solution.py:49
  23.2 505.0 %while.18 = (s32[]{:T(128)}, f32[2,3,2,512,128]{4,3,2,1,0:T(8,128)S(1)}, f32[2,3,2,512,128]{4,3,2,1,0:T(8,128)}, f32[2,3,2,512,128]{4,3,2,1,0:T(8,128)}, f32[2,3...) while((s32[]{:T(128)}, ...), condition=%wide.region_1.2_spmd.clone, body=%wide.region_0.1_spmd.clone.sunk | while | flops 24124420 | bytes 196016720 | solution.py:111
  31.5 5.7 %multiply_add_fusion.7 = (f32[2,3,2,512,128]{4,3,2,1,0:T(8,128)}, f32[2,3,2,512,128]{4,3,2,1,0:T(8,128)S(1)}) fusion(f32[2,3,2,512,128]{4,3,2,1,0:T(8,128)} %get-tuple-element.473, pred[]{:T(512)S(6)} %compare.7, f32[2,3,2,512,128]{4,3,2,1,0:T(8,128)S(1)} %get-tuple-element.471, f32[2,512,128]{2,1,0:T(8,128)S(1)} %copy-done.8, ...), kind=kLoop, calls=%fused_computation.8.clone.1 | loop fusion | flops 7077888 | bytes 17301504 | tf_op jit(solution)/shard_map/while/body/eval_jaxpr/add | solution.py:73
  37.2 2.7 collective-permute-done
  47.5 11.3 %collective-permute-done.1 = f32[2,2,1,512,128]{4,3,2,1,0:T(8,128)S(1)} collective-permute-done((f32[2,2,1,512,128]{4,3,2,1,0:T(8,128)S(1)}, f32[2,2,1,512,128]{4,3,2,1,0:T(8,128)S(1)}, u32[]{:S(2)}, u32[]{:S(2)}) %collective-permute-start.1) | collective-permute-done | bytes 1048608 | tf_op jit(solution)/shard_map/while/body/eval_jaxpr/ppermute | solution.py:17
  63.1 8.0 %collective-permute-start = (f32[2,2,1,512,128]{4,3,0,2,1:T(8,128)}, f32[2,2,1,512,128]{4,3,0,2,1:T(8,128)}, u32[]{:S(2)}, u32[]{:S(2)}) collective-permute-start(f32[2,2,1,512,128]{4,3,0,2,1:T(8,128)} %slice.472), channel_id=1, source_target_pairs={{0,15},{1,0},{2,1},{3,2},{4,3},{5,4},{6,5},{7,6},{8,7},{9,8},{10,9... | collective-permute-start | bytes 3145736 | tf_op jit(solution)/shard_map/while/body/eval_jaxpr/ppermute | solution.py:17
  78.1 6.7 %multiply_add_fusion.7 = (f32[2,3,2,512,128]{4,3,2,1,0:T(8,128)}, f32[2,3,2,512,128]{4,3,2,1,0:T(8,128)S(1)}) fusion(f32[2,3,2,512,128]{4,3,2,1,0:T(8,128)} %get-tuple-element.473, pred[]{:T(512)S(6)} %compare.7, f32[2,3,2,512,128]{4,3,2,1,0:T(8,128)S(1)} %get-tuple-element.471, f32[2,512,128]{2,1,0:T(8,128)S(1)} %copy-done.8, ...), kind=kLoop, calls=%fused_computation.8.clone.1 | loop fusion | flops 7077888 | bytes 17301504 | tf_op jit(solution)/shard_map/while/body/eval_jaxpr/add | solution.py:73
  84.8 2.1 multiply_subtract_fusion.10
  92.5 11.3 %collective-permute-done.1 = f32[2,2,1,512,128]{4,3,2,1,0:T(8,128)S(1)} collective-permute-done((f32[2,2,1,512,128]{4,3,2,1,0:T(8,128)S(1)}, f32[2,2,1,512,128]{4,3,2,1,0:T(8,128)S(1)}, u32[]{:S(2)}, u32[]{:S(2)}) %collective-permute-start.1) | collective-permute-done | bytes 1048608 | tf_op jit(solution)/shard_map/while/body/eval_jaxpr/ppermute | solution.py:17
  108.1 5.2 collective-permute-start
  120.3 6.7 %multiply_add_fusion.7 = (f32[2,3,2,512,128]{4,3,2,1,0:T(8,128)}, f32[2,3,2,512,128]{4,3,2,1,0:T(8,128)S(1)}) fusion(f32[2,3,2,512,128]{4,3,2,1,0:T(8,128)} %get-tuple-element.473, pred[]{:T(512)S(6)} %compare.7, f32[2,3,2,512,128]{4,3,2,1,0:T(8,128)S(1)} %get-tuple-element.471, f32[2,512,128]{2,1,0:T(8,128)S(1)} %copy-done.8, ...), kind=kLoop, calls=%fused_computation.8.clone.1 | loop fusion | flops 7077888 | bytes 17301504 | tf_op jit(solution)/shard_map/while/body/eval_jaxpr/add | solution.py:73
  126.9 2.1 multiply_subtract_fusion.10
  134.6 11.3 %collective-permute-done.1 = f32[2,2,1,512,128]{4,3,2,1,0:T(8,128)S(1)} collective-permute-done((f32[2,2,1,512,128]{4,3,2,1,0:T(8,128)S(1)}, f32[2,2,1,512,128]{4,3,2,1,0:T(8,128)S(1)}, u32[]{:S(2)}, u32[]{:S(2)}) %collective-permute-start.1) | collective-permute-done | bytes 1048608 | tf_op jit(solution)/shard_map/while/body/eval_jaxpr/ppermute | solution.py:17
  150.2 5.2 collective-permute-start
  162.4 6.7 %multiply_add_fusion.7 = (f32[2,3,2,512,128]{4,3,2,1,0:T(8,128)}, f32[2,3,2,512,128]{4,3,2,1,0:T(8,128)S(1)}) fusion(f32[2,3,2,512,128]{4,3,2,1,0:T(8,128)} %get-tuple-element.473, pred[]{:T(512)S(6)} %compare.7, f32[2,3,2,512,128]{4,3,2,1,0:T(8,128)S(1)} %get-tuple-element.471, f32[2,512,128]{2,1,0:T(8,128)S(1)} %copy-done.8, ...), kind=kLoop, calls=%fused_computation.8.clone.1 | loop fusion | flops 7077888 | bytes 17301504 | tf_op jit(solution)/shard_map/while/body/eval_jaxpr/add | solution.py:73
  169.1 2.1 multiply_subtract_fusion.10
  176.8 11.3 %collective-permute-done.1 = f32[2,2,1,512,128]{4,3,2,1,0:T(8,128)S(1)} collective-permute-done((f32[2,2,1,512,128]{4,3,2,1,0:T(8,128)S(1)}, f32[2,2,1,512,128]{4,3,2,1,0:T(8,128)S(1)}, u32[]{:S(2)}, u32[]{:S(2)}) %collective-permute-start.1) | collective-permute-done | bytes 1048608 | tf_op jit(solution)/shard_map/while/body/eval_jaxpr/ppermute | solution.py:17
  192.3 5.2 collective-permute-start
  204.5 6.7 %multiply_add_fusion.7 = (f32[2,3,2,512,128]{4,3,2,1,0:T(8,128)}, f32[2,3,2,512,128]{4,3,2,1,0:T(8,128)S(1)}) fusion(f32[2,3,2,512,128]{4,3,2,1,0:T(8,128)} %get-tuple-element.473, pred[]{:T(512)S(6)} %compare.7, f32[2,3,2,512,128]{4,3,2,1,0:T(8,128)S(1)} %get-tuple-element.471, f32[2,512,128]{2,1,0:T(8,128)S(1)} %copy-done.8, ...), kind=kLoop, calls=%fused_computation.8.clone.1 | loop fusion | flops 7077888 | bytes 17301504 | tf_op jit(solution)/shard_map/while/body/eval_jaxpr/add | solution.py:73
  211.2 2.1 multiply_subtract_fusion.10
  218.9 11.3 %collective-permute-done.1 = f32[2,2,1,512,128]{4,3,2,1,0:T(8,128)S(1)} collective-permute-done((f32[2,2,1,512,128]{4,3,2,1,0:T(8,128)S(1)}, f32[2,2,1,512,128]{4,3,2,1,0:T(8,128)S(1)}, u32[]{:S(2)}, u32[]{:S(2)}) %collective-permute-start.1) | collective-permute-done | bytes 1048608 | tf_op jit(solution)/shard_map/while/body/eval_jaxpr/ppermute | solution.py:17
  234.5 5.2 collective-permute-start
  246.7 6.7 %multiply_add_fusion.7 = (f32[2,3,2,512,128]{4,3,2,1,0:T(8,128)}, f32[2,3,2,512,128]{4,3,2,1,0:T(8,128)S(1)}) fusion(f32[2,3,2,512,128]{4,3,2,1,0:T(8,128)} %get-tuple-element.473, pred[]{:T(512)S(6)} %compare.7, f32[2,3,2,512,128]{4,3,2,1,0:T(8,128)S(1)} %get-tuple-element.471, f32[2,512,128]{2,1,0:T(8,128)S(1)} %copy-done.8, ...), kind=kLoop, calls=%fused_computation.8.clone.1 | loop fusion | flops 7077888 | bytes 17301504 | tf_op jit(solution)/shard_map/while/body/eval_jaxpr/add | solution.py:73
  253.3 2.1 multiply_subtract_fusion.10
  261.0 11.3 %collective-permute-done.1 = f32[2,2,1,512,128]{4,3,2,1,0:T(8,128)S(1)} collective-permute-done((f32[2,2,1,512,128]{4,3,2,1,0:T(8,128)S(1)}, f32[2,2,1,512,128]{4,3,2,1,0:T(8,128)S(1)}, u32[]{:S(2)}, u32[]{:S(2)}) %collective-permute-start.1) | collective-permute-done | bytes 1048608 | tf_op jit(solution)/shard_map/while/body/eval_jaxpr/ppermute | solution.py:17
  276.6 5.2 collective-permute-start
  288.8 6.7 %multiply_add_fusion.7 = (f32[2,3,2,512,128]{4,3,2,1,0:T(8,128)}, f32[2,3,2,512,128]{4,3,2,1,0:T(8,128)S(1)}) fusion(f32[2,3,2,512,128]{4,3,2,1,0:T(8,128)} %get-tuple-element.473, pred[]{:T(512)S(6)} %compare.7, f32[2,3,2,512,128]{4,3,2,1,0:T(8,128)S(1)} %get-tuple-element.471, f32[2,512,128]{2,1,0:T(8,128)S(1)} %copy-done.8, ...), kind=kLoop, calls=%fused_computation.8.clone.1 | loop fusion | flops 7077888 | bytes 17301504 | tf_op jit(solution)/shard_map/while/body/eval_jaxpr/add | solution.py:73
  295.5 2.1 multiply_subtract_fusion.10
  303.2 11.3 %collective-permute-done.1 = f32[2,2,1,512,128]{4,3,2,1,0:T(8,128)S(1)} collective-permute-done((f32[2,2,1,512,128]{4,3,2,1,0:T(8,128)S(1)}, f32[2,2,1,512,128]{4,3,2,1,0:T(8,128)S(1)}, u32[]{:S(2)}, u32[]{:S(2)}) %collective-permute-start.1) | collective-permute-done | bytes 1048608 | tf_op jit(solution)/shard_map/while/body/eval_jaxpr/ppermute | solution.py:17
  318.7 5.2 collective-permute-start
  330.9 6.7 %multiply_add_fusion.7 = (f32[2,3,2,512,128]{4,3,2,1,0:T(8,128)}, f32[2,3,2,512,128]{4,3,2,1,0:T(8,128)S(1)}) fusion(f32[2,3,2,512,128]{4,3,2,1,0:T(8,128)} %get-tuple-element.473, pred[]{:T(512)S(6)} %compare.7, f32[2,3,2,512,128]{4,3,2,1,0:T(8,128)S(1)} %get-tuple-element.471, f32[2,512,128]{2,1,0:T(8,128)S(1)} %copy-done.8, ...), kind=kLoop, calls=%fused_computation.8.clone.1 | loop fusion | flops 7077888 | bytes 17301504 | tf_op jit(solution)/shard_map/while/body/eval_jaxpr/add | solution.py:73
  345.3 11.3 %collective-permute-done.1 = f32[2,2,1,512,128]{4,3,2,1,0:T(8,128)S(1)} collective-permute-done((f32[2,2,1,512,128]{4,3,2,1,0:T(8,128)S(1)}, f32[2,2,1,512,128]{4,3,2,1,0:T(8,128)S(1)}, u32[]{:S(2)}, u32[]{:S(2)}) %collective-permute-start.1) | collective-permute-done | bytes 1048608 | tf_op jit(solution)/shard_map/while/body/eval_jaxpr/ppermute | solution.py:17
  360.9 5.2 collective-permute-start
  373.1 6.7 %multiply_add_fusion.7 = (f32[2,3,2,512,128]{4,3,2,1,0:T(8,128)}, f32[2,3,2,512,128]{4,3,2,1,0:T(8,128)S(1)}) fusion(f32[2,3,2,512,128]{4,3,2,1,0:T(8,128)} %get-tuple-element.473, pred[]{:T(512)S(6)} %compare.7, f32[2,3,2,512,128]{4,3,2,1,0:T(8,128)S(1)} %get-tuple-element.471, f32[2,512,128]{2,1,0:T(8,128)S(1)} %copy-done.8, ...), kind=kLoop, calls=%fused_computation.8.clone.1 | loop fusion | flops 7077888 | bytes 17301504 | tf_op jit(solution)/shard_map/while/body/eval_jaxpr/add | solution.py:73
  379.7 2.1 multiply_subtract_fusion.10
  387.4 11.3 %collective-permute-done.1 = f32[2,2,1,512,128]{4,3,2,1,0:T(8,128)S(1)} collective-permute-done((f32[2,2,1,512,128]{4,3,2,1,0:T(8,128)S(1)}, f32[2,2,1,512,128]{4,3,2,1,0:T(8,128)S(1)}, u32[]{:S(2)}, u32[]{:S(2)}) %collective-permute-start.1) | collective-permute-done | bytes 1048608 | tf_op jit(solution)/shard_map/while/body/eval_jaxpr/ppermute | solution.py:17
  403.0 5.2 collective-permute-start
  415.2 6.7 %multiply_add_fusion.7 = (f32[2,3,2,512,128]{4,3,2,1,0:T(8,128)}, f32[2,3,2,512,128]{4,3,2,1,0:T(8,128)S(1)}) fusion(f32[2,3,2,512,128]{4,3,2,1,0:T(8,128)} %get-tuple-element.473, pred[]{:T(512)S(6)} %compare.7, f32[2,3,2,512,128]{4,3,2,1,0:T(8,128)S(1)} %get-tuple-element.471, f32[2,512,128]{2,1,0:T(8,128)S(1)} %copy-done.8, ...), kind=kLoop, calls=%fused_computation.8.clone.1 | loop fusion | flops 7077888 | bytes 17301504 | tf_op jit(solution)/shard_map/while/body/eval_jaxpr/add | solution.py:73
  429.6 11.3 %collective-permute-done.1 = f32[2,2,1,512,128]{4,3,2,1,0:T(8,128)S(1)} collective-permute-done((f32[2,2,1,512,128]{4,3,2,1,0:T(8,128)S(1)}, f32[2,2,1,512,128]{4,3,2,1,0:T(8,128)S(1)}, u32[]{:S(2)}, u32[]{:S(2)}) %collective-permute-start.1) | collective-permute-done | bytes 1048608 | tf_op jit(solution)/shard_map/while/body/eval_jaxpr/ppermute | solution.py:17
  445.1 5.2 collective-permute-start
  457.3 6.7 %multiply_add_fusion.7 = (f32[2,3,2,512,128]{4,3,2,1,0:T(8,128)}, f32[2,3,2,512,128]{4,3,2,1,0:T(8,128)S(1)}) fusion(f32[2,3,2,512,128]{4,3,2,1,0:T(8,128)} %get-tuple-element.473, pred[]{:T(512)S(6)} %compare.7, f32[2,3,2,512,128]{4,3,2,1,0:T(8,128)S(1)} %get-tuple-element.471, f32[2,512,128]{2,1,0:T(8,128)S(1)} %copy-done.8, ...), kind=kLoop, calls=%fused_computation.8.clone.1 | loop fusion | flops 7077888 | bytes 17301504 | tf_op jit(solution)/shard_map/while/body/eval_jaxpr/add | solution.py:73
  464.0 2.1 multiply_subtract_fusion.10
  471.7 11.3 %collective-permute-done.1 = f32[2,2,1,512,128]{4,3,2,1,0:T(8,128)S(1)} collective-permute-done((f32[2,2,1,512,128]{4,3,2,1,0:T(8,128)S(1)}, f32[2,2,1,512,128]{4,3,2,1,0:T(8,128)S(1)}, u32[]{:S(2)}, u32[]{:S(2)}) %collective-permute-start.1) | collective-permute-done | bytes 1048608 | tf_op jit(solution)/shard_map/while/body/eval_jaxpr/ppermute | solution.py:17
  487.3 5.2 collective-permute-start
  499.5 6.7 %multiply_add_fusion.7 = (f32[2,3,2,512,128]{4,3,2,1,0:T(8,128)}, f32[2,3,2,512,128]{4,3,2,1,0:T(8,128)S(1)}) fusion(f32[2,3,2,512,128]{4,3,2,1,0:T(8,128)} %get-tuple-element.473, pred[]{:T(512)S(6)} %compare.7, f32[2,3,2,512,128]{4,3,2,1,0:T(8,128)S(1)} %get-tuple-element.471, f32[2,512,128]{2,1,0:T(8,128)S(1)} %copy-done.8, ...), kind=kLoop, calls=%fused_computation.8.clone.1 | loop fusion | flops 7077888 | bytes 17301504 | tf_op jit(solution)/shard_map/while/body/eval_jaxpr/add | solution.py:73
  513.8 11.3 %collective-permute-done.1 = f32[2,2,1,512,128]{4,3,2,1,0:T(8,128)S(1)} collective-permute-done((f32[2,2,1,512,128]{4,3,2,1,0:T(8,128)S(1)}, f32[2,2,1,512,128]{4,3,2,1,0:T(8,128)S(1)}, u32[]{:S(2)}, u32[]{:S(2)}) %collective-permute-start.1) | collective-permute-done | bytes 1048608 | tf_op jit(solution)/shard_map/while/body/eval_jaxpr/ppermute | solution.py:17
  (662 shorter events, 213.0 us)
Async XLA Ops:
  4.4 18.8 %copy-start.1 = (f32[2,3,2,512,128]{4,3,2,1,0:T(8,128)S(1)}, f32[2,3,2,512,128]{4,3,2,1,0:T(8,128)}, u32[]{:S(2)}) copy-start(f32[2,3,2,512,128]{4,3,2,1,0:T(8,128)} %param.10) | copy-start | bytes 9437188
  24.4 15.4 %collective-permute-start = (f32[2,2,1,512,128]{4,3,0,2,1:T(8,128)}, f32[2,2,1,512,128]{4,3,0,2,1:T(8,128)}, u32[]{:S(2)}, u32[]{:S(2)}) collective-permute-start(f32[2,2,1,512,128]{4,3,0,2,1:T(8,128)} %slice.472), channel_id=1, source_target_pairs={{0,15},{1,0},{2,1},{3,2},{4,3},{5,4},{6,5},{7,6},{8,7},{9,8},{10,9... | collective-permute-start | bytes 3145736 | tf_op jit(solution)/shard_map/while/body/eval_jaxpr/ppermute | solution.py:17
  37.2 23.1 %copy-start.5 = (f32[2,3,2,512,128]{4,3,2,1,0:T(8,128)}, f32[2,3,2,512,128]{4,3,2,1,0:T(8,128)S(1)}, u32[]{:S(2)}) copy-start(f32[2,3,2,512,128]{4,3,2,1,0:T(8,128)S(1)} %get-tuple-element.493) | copy-start | bytes 9437188 | tf_op jit(solution)/shard_map/while
  46.2 13.2 %copy-start.3 = (f32[2,3,2,512,128]{4,3,2,1,0:T(8,128)}, f32[2,3,2,512,128]{4,3,2,1,0:T(8,128)S(1)}, u32[]{:S(2)}) copy-start(f32[2,3,2,512,128]{4,3,2,1,0:T(8,128)S(1)} %fusion.58) | copy-start | bytes 9437188 | tf_op jit(solution)/shard_map/while
  46.3 12.5 %collective-permute-start.1 = (f32[2,2,1,512,128]{4,3,2,1,0:T(8,128)S(1)}, f32[2,2,1,512,128]{4,3,2,1,0:T(8,128)S(1)}, u32[]{:S(2)}, u32[]{:S(2)}) collective-permute-start(f32[2,2,1,512,128]{4,3,2,1,0:T(8,128)S(1)} %slice.477), channel_id=1, source_target_pairs={{0,1},{1,2},{2,3},{3,4},{4,5},{5,6},{6,7},{7,8},{8,9},{9,10},{10,1... | collective-permute-start | bytes 3145736 | tf_op jit(solution)/shard_map/while/body/eval_jaxpr/ppermute | solution.py:17
  63.1 21.7 %collective-permute-start = (f32[2,2,1,512,128]{4,3,0,2,1:T(8,128)}, f32[2,2,1,512,128]{4,3,0,2,1:T(8,128)}, u32[]{:S(2)}, u32[]{:S(2)}) collective-permute-start(f32[2,2,1,512,128]{4,3,0,2,1:T(8,128)} %slice.472), channel_id=1, source_target_pairs={{0,15},{1,0},{2,1},{3,2},{4,3},{5,4},{6,5},{7,6},{8,7},{9,8},{10,9... | collective-permute-start | bytes 3145736 | tf_op jit(solution)/shard_map/while/body/eval_jaxpr/ppermute | solution.py:17
  84.8 20.5 %copy-start.5 = (f32[2,3,2,512,128]{4,3,2,1,0:T(8,128)}, f32[2,3,2,512,128]{4,3,2,1,0:T(8,128)S(1)}, u32[]{:S(2)}) copy-start(f32[2,3,2,512,128]{4,3,2,1,0:T(8,128)S(1)} %get-tuple-element.493) | copy-start | bytes 9437188 | tf_op jit(solution)/shard_map/while
  91.9 12.5 %copy-start.3 = (f32[2,3,2,512,128]{4,3,2,1,0:T(8,128)}, f32[2,3,2,512,128]{4,3,2,1,0:T(8,128)S(1)}, u32[]{:S(2)}) copy-start(f32[2,3,2,512,128]{4,3,2,1,0:T(8,128)S(1)} %fusion.58) | copy-start | bytes 9437188 | tf_op jit(solution)/shard_map/while
  92.0 11.8 %collective-permute-start.1 = (f32[2,2,1,512,128]{4,3,2,1,0:T(8,128)S(1)}, f32[2,2,1,512,128]{4,3,2,1,0:T(8,128)S(1)}, u32[]{:S(2)}, u32[]{:S(2)}) collective-permute-start(f32[2,2,1,512,128]{4,3,2,1,0:T(8,128)S(1)} %slice.477), channel_id=1, source_target_pairs={{0,1},{1,2},{2,3},{3,4},{4,5},{5,6},{6,7},{7,8},{8,9},{9,10},{10,1... | collective-permute-start | bytes 3145736 | tf_op jit(solution)/shard_map/while/body/eval_jaxpr/ppermute | solution.py:17
  108.1 18.9 %collective-permute-start = (f32[2,2,1,512,128]{4,3,0,2,1:T(8,128)}, f32[2,2,1,512,128]{4,3,0,2,1:T(8,128)}, u32[]{:S(2)}, u32[]{:S(2)}) collective-permute-start(f32[2,2,1,512,128]{4,3,0,2,1:T(8,128)} %slice.472), channel_id=1, source_target_pairs={{0,15},{1,0},{2,1},{3,2},{4,3},{5,4},{6,5},{7,6},{8,7},{9,8},{10,9... | collective-permute-start | bytes 3145736 | tf_op jit(solution)/shard_map/while/body/eval_jaxpr/ppermute | solution.py:17
  126.9 20.5 %copy-start.5 = (f32[2,3,2,512,128]{4,3,2,1,0:T(8,128)}, f32[2,3,2,512,128]{4,3,2,1,0:T(8,128)S(1)}, u32[]{:S(2)}) copy-start(f32[2,3,2,512,128]{4,3,2,1,0:T(8,128)S(1)} %get-tuple-element.493) | copy-start | bytes 9437188 | tf_op jit(solution)/shard_map/while
  134.1 12.5 %copy-start.3 = (f32[2,3,2,512,128]{4,3,2,1,0:T(8,128)}, f32[2,3,2,512,128]{4,3,2,1,0:T(8,128)S(1)}, u32[]{:S(2)}) copy-start(f32[2,3,2,512,128]{4,3,2,1,0:T(8,128)S(1)} %fusion.58) | copy-start | bytes 9437188 | tf_op jit(solution)/shard_map/while
  134.1 11.8 %collective-permute-start.1 = (f32[2,2,1,512,128]{4,3,2,1,0:T(8,128)S(1)}, f32[2,2,1,512,128]{4,3,2,1,0:T(8,128)S(1)}, u32[]{:S(2)}, u32[]{:S(2)}) collective-permute-start(f32[2,2,1,512,128]{4,3,2,1,0:T(8,128)S(1)} %slice.477), channel_id=1, source_target_pairs={{0,1},{1,2},{2,3},{3,4},{4,5},{5,6},{6,7},{7,8},{8,9},{9,10},{10,1... | collective-permute-start | bytes 3145736 | tf_op jit(solution)/shard_map/while/body/eval_jaxpr/ppermute | solution.py:17
  150.2 18.9 %collective-permute-start = (f32[2,2,1,512,128]{4,3,0,2,1:T(8,128)}, f32[2,2,1,512,128]{4,3,0,2,1:T(8,128)}, u32[]{:S(2)}, u32[]{:S(2)}) collective-permute-start(f32[2,2,1,512,128]{4,3,0,2,1:T(8,128)} %slice.472), channel_id=1, source_target_pairs={{0,15},{1,0},{2,1},{3,2},{4,3},{5,4},{6,5},{7,6},{8,7},{9,8},{10,9... | collective-permute-start | bytes 3145736 | tf_op jit(solution)/shard_map/while/body/eval_jaxpr/ppermute | solution.py:17
  169.1 20.5 %copy-start.5 = (f32[2,3,2,512,128]{4,3,2,1,0:T(8,128)}, f32[2,3,2,512,128]{4,3,2,1,0:T(8,128)S(1)}, u32[]{:S(2)}) copy-start(f32[2,3,2,512,128]{4,3,2,1,0:T(8,128)S(1)} %get-tuple-element.493) | copy-start | bytes 9437188 | tf_op jit(solution)/shard_map/while
  176.2 12.5 %copy-start.3 = (f32[2,3,2,512,128]{4,3,2,1,0:T(8,128)}, f32[2,3,2,512,128]{4,3,2,1,0:T(8,128)S(1)}, u32[]{:S(2)}) copy-start(f32[2,3,2,512,128]{4,3,2,1,0:T(8,128)S(1)} %fusion.58) | copy-start | bytes 9437188 | tf_op jit(solution)/shard_map/while
  176.3 11.8 %collective-permute-start.1 = (f32[2,2,1,512,128]{4,3,2,1,0:T(8,128)S(1)}, f32[2,2,1,512,128]{4,3,2,1,0:T(8,128)S(1)}, u32[]{:S(2)}, u32[]{:S(2)}) collective-permute-start(f32[2,2,1,512,128]{4,3,2,1,0:T(8,128)S(1)} %slice.477), channel_id=1, source_target_pairs={{0,1},{1,2},{2,3},{3,4},{4,5},{5,6},{6,7},{7,8},{8,9},{9,10},{10,1... | collective-permute-start | bytes 3145736 | tf_op jit(solution)/shard_map/while/body/eval_jaxpr/ppermute | solution.py:17
  192.3 18.9 %collective-permute-start = (f32[2,2,1,512,128]{4,3,0,2,1:T(8,128)}, f32[2,2,1,512,128]{4,3,0,2,1:T(8,128)}, u32[]{:S(2)}, u32[]{:S(2)}) collective-permute-start(f32[2,2,1,512,128]{4,3,0,2,1:T(8,128)} %slice.472), channel_id=1, source_target_pairs={{0,15},{1,0},{2,1},{3,2},{4,3},{5,4},{6,5},{7,6},{8,7},{9,8},{10,9... | collective-permute-start | bytes 3145736 | tf_op jit(solution)/shard_map/while/body/eval_jaxpr/ppermute | solution.py:17
  211.2 20.5 %copy-start.5 = (f32[2,3,2,512,128]{4,3,2,1,0:T(8,128)}, f32[2,3,2,512,128]{4,3,2,1,0:T(8,128)S(1)}, u32[]{:S(2)}) copy-start(f32[2,3,2,512,128]{4,3,2,1,0:T(8,128)S(1)} %get-tuple-element.493) | copy-start | bytes 9437188 | tf_op jit(solution)/shard_map/while
  218.3 12.5 %copy-start.3 = (f32[2,3,2,512,128]{4,3,2,1,0:T(8,128)}, f32[2,3,2,512,128]{4,3,2,1,0:T(8,128)S(1)}, u32[]{:S(2)}) copy-start(f32[2,3,2,512,128]{4,3,2,1,0:T(8,128)S(1)} %fusion.58) | copy-start | bytes 9437188 | tf_op jit(solution)/shard_map/while
  218.4 11.8 %collective-permute-start.1 = (f32[2,2,1,512,128]{4,3,2,1,0:T(8,128)S(1)}, f32[2,2,1,512,128]{4,3,2,1,0:T(8,128)S(1)}, u32[]{:S(2)}, u32[]{:S(2)}) collective-permute-start(f32[2,2,1,512,128]{4,3,2,1,0:T(8,128)S(1)} %slice.477), channel_id=1, source_target_pairs={{0,1},{1,2},{2,3},{3,4},{4,5},{5,6},{6,7},{7,8},{8,9},{9,10},{10,1... | collective-permute-start | bytes 3145736 | tf_op jit(solution)/shard_map/while/body/eval_jaxpr/ppermute | solution.py:17
  234.5 18.9 %collective-permute-start = (f32[2,2,1,512,128]{4,3,0,2,1:T(8,128)}, f32[2,2,1,512,128]{4,3,0,2,1:T(8,128)}, u32[]{:S(2)}, u32[]{:S(2)}) collective-permute-start(f32[2,2,1,512,128]{4,3,0,2,1:T(8,128)} %slice.472), channel_id=1, source_target_pairs={{0,15},{1,0},{2,1},{3,2},{4,3},{5,4},{6,5},{7,6},{8,7},{9,8},{10,9... | collective-permute-start | bytes 3145736 | tf_op jit(solution)/shard_map/while/body/eval_jaxpr/ppermute | solution.py:17
  253.3 20.5 %copy-start.5 = (f32[2,3,2,512,128]{4,3,2,1,0:T(8,128)}, f32[2,3,2,512,128]{4,3,2,1,0:T(8,128)S(1)}, u32[]{:S(2)}) copy-start(f32[2,3,2,512,128]{4,3,2,1,0:T(8,128)S(1)} %get-tuple-element.493) | copy-start | bytes 9437188 | tf_op jit(solution)/shard_map/while
  260.5 12.5 %copy-start.3 = (f32[2,3,2,512,128]{4,3,2,1,0:T(8,128)}, f32[2,3,2,512,128]{4,3,2,1,0:T(8,128)S(1)}, u32[]{:S(2)}) copy-start(f32[2,3,2,512,128]{4,3,2,1,0:T(8,128)S(1)} %fusion.58) | copy-start | bytes 9437188 | tf_op jit(solution)/shard_map/while
  260.5 11.8 %collective-permute-start.1 = (f32[2,2,1,512,128]{4,3,2,1,0:T(8,128)S(1)}, f32[2,2,1,512,128]{4,3,2,1,0:T(8,128)S(1)}, u32[]{:S(2)}, u32[]{:S(2)}) collective-permute-start(f32[2,2,1,512,128]{4,3,2,1,0:T(8,128)S(1)} %slice.477), channel_id=1, source_target_pairs={{0,1},{1,2},{2,3},{3,4},{4,5},{5,6},{6,7},{7,8},{8,9},{9,10},{10,1... | collective-permute-start | bytes 3145736 | tf_op jit(solution)/shard_map/while/body/eval_jaxpr/ppermute | solution.py:17
  276.6 18.9 %collective-permute-start = (f32[2,2,1,512,128]{4,3,0,2,1:T(8,128)}, f32[2,2,1,512,128]{4,3,0,2,1:T(8,128)}, u32[]{:S(2)}, u32[]{:S(2)}) collective-permute-start(f32[2,2,1,512,128]{4,3,0,2,1:T(8,128)} %slice.472), channel_id=1, source_target_pairs={{0,15},{1,0},{2,1},{3,2},{4,3},{5,4},{6,5},{7,6},{8,7},{9,8},{10,9... | collective-permute-start | bytes 3145736 | tf_op jit(solution)/shard_map/while/body/eval_jaxpr/ppermute | solution.py:17
  295.5 20.5 %copy-start.5 = (f32[2,3,2,512,128]{4,3,2,1,0:T(8,128)}, f32[2,3,2,512,128]{4,3,2,1,0:T(8,128)S(1)}, u32[]{:S(2)}) copy-start(f32[2,3,2,512,128]{4,3,2,1,0:T(8,128)S(1)} %get-tuple-element.493) | copy-start | bytes 9437188 | tf_op jit(solution)/shard_map/while
  302.6 12.5 %copy-start.3 = (f32[2,3,2,512,128]{4,3,2,1,0:T(8,128)}, f32[2,3,2,512,128]{4,3,2,1,0:T(8,128)S(1)}, u32[]{:S(2)}) copy-start(f32[2,3,2,512,128]{4,3,2,1,0:T(8,128)S(1)} %fusion.58) | copy-start | bytes 9437188 | tf_op jit(solution)/shard_map/while
  302.7 11.8 %collective-permute-start.1 = (f32[2,2,1,512,128]{4,3,2,1,0:T(8,128)S(1)}, f32[2,2,1,512,128]{4,3,2,1,0:T(8,128)S(1)}, u32[]{:S(2)}, u32[]{:S(2)}) collective-permute-start(f32[2,2,1,512,128]{4,3,2,1,0:T(8,128)S(1)} %slice.477), channel_id=1, source_target_pairs={{0,1},{1,2},{2,3},{3,4},{4,5},{5,6},{6,7},{7,8},{8,9},{9,10},{10,1... | collective-permute-start | bytes 3145736 | tf_op jit(solution)/shard_map/while/body/eval_jaxpr/ppermute | solution.py:17
  318.7 18.9 %collective-permute-start = (f32[2,2,1,512,128]{4,3,0,2,1:T(8,128)}, f32[2,2,1,512,128]{4,3,0,2,1:T(8,128)}, u32[]{:S(2)}, u32[]{:S(2)}) collective-permute-start(f32[2,2,1,512,128]{4,3,0,2,1:T(8,128)} %slice.472), channel_id=1, source_target_pairs={{0,15},{1,0},{2,1},{3,2},{4,3},{5,4},{6,5},{7,6},{8,7},{9,8},{10,9... | collective-permute-start | bytes 3145736 | tf_op jit(solution)/shard_map/while/body/eval_jaxpr/ppermute | solution.py:17
  337.6 20.5 %copy-start.5 = (f32[2,3,2,512,128]{4,3,2,1,0:T(8,128)}, f32[2,3,2,512,128]{4,3,2,1,0:T(8,128)S(1)}, u32[]{:S(2)}) copy-start(f32[2,3,2,512,128]{4,3,2,1,0:T(8,128)S(1)} %get-tuple-element.493) | copy-start | bytes 9437188 | tf_op jit(solution)/shard_map/while
  344.7 12.5 %copy-start.3 = (f32[2,3,2,512,128]{4,3,2,1,0:T(8,128)}, f32[2,3,2,512,128]{4,3,2,1,0:T(8,128)S(1)}, u32[]{:S(2)}) copy-start(f32[2,3,2,512,128]{4,3,2,1,0:T(8,128)S(1)} %fusion.58) | copy-start | bytes 9437188 | tf_op jit(solution)/shard_map/while
  344.8 11.8 %collective-permute-start.1 = (f32[2,2,1,512,128]{4,3,2,1,0:T(8,128)S(1)}, f32[2,2,1,512,128]{4,3,2,1,0:T(8,128)S(1)}, u32[]{:S(2)}, u32[]{:S(2)}) collective-permute-start(f32[2,2,1,512,128]{4,3,2,1,0:T(8,128)S(1)} %slice.477), channel_id=1, source_target_pairs={{0,1},{1,2},{2,3},{3,4},{4,5},{5,6},{6,7},{7,8},{8,9},{9,10},{10,1... | collective-permute-start | bytes 3145736 | tf_op jit(solution)/shard_map/while/body/eval_jaxpr/ppermute | solution.py:17
  360.9 18.9 %collective-permute-start = (f32[2,2,1,512,128]{4,3,0,2,1:T(8,128)}, f32[2,2,1,512,128]{4,3,0,2,1:T(8,128)}, u32[]{:S(2)}, u32[]{:S(2)}) collective-permute-start(f32[2,2,1,512,128]{4,3,0,2,1:T(8,128)} %slice.472), channel_id=1, source_target_pairs={{0,15},{1,0},{2,1},{3,2},{4,3},{5,4},{6,5},{7,6},{8,7},{9,8},{10,9... | collective-permute-start | bytes 3145736 | tf_op jit(solution)/shard_map/while/body/eval_jaxpr/ppermute | solution.py:17
  379.7 20.5 %copy-start.5 = (f32[2,3,2,512,128]{4,3,2,1,0:T(8,128)}, f32[2,3,2,512,128]{4,3,2,1,0:T(8,128)S(1)}, u32[]{:S(2)}) copy-start(f32[2,3,2,512,128]{4,3,2,1,0:T(8,128)S(1)} %get-tuple-element.493) | copy-start | bytes 9437188 | tf_op jit(solution)/shard_map/while
  386.9 12.5 %copy-start.3 = (f32[2,3,2,512,128]{4,3,2,1,0:T(8,128)}, f32[2,3,2,512,128]{4,3,2,1,0:T(8,128)S(1)}, u32[]{:S(2)}) copy-start(f32[2,3,2,512,128]{4,3,2,1,0:T(8,128)S(1)} %fusion.58) | copy-start | bytes 9437188 | tf_op jit(solution)/shard_map/while
  386.9 11.8 %collective-permute-start.1 = (f32[2,2,1,512,128]{4,3,2,1,0:T(8,128)S(1)}, f32[2,2,1,512,128]{4,3,2,1,0:T(8,128)S(1)}, u32[]{:S(2)}, u32[]{:S(2)}) collective-permute-start(f32[2,2,1,512,128]{4,3,2,1,0:T(8,128)S(1)} %slice.477), channel_id=1, source_target_pairs={{0,1},{1,2},{2,3},{3,4},{4,5},{5,6},{6,7},{7,8},{8,9},{9,10},{10,1... | collective-permute-start | bytes 3145736 | tf_op jit(solution)/shard_map/while/body/eval_jaxpr/ppermute | solution.py:17
  403.0 18.9 %collective-permute-start = (f32[2,2,1,512,128]{4,3,0,2,1:T(8,128)}, f32[2,2,1,512,128]{4,3,0,2,1:T(8,128)}, u32[]{:S(2)}, u32[]{:S(2)}) collective-permute-start(f32[2,2,1,512,128]{4,3,0,2,1:T(8,128)} %slice.472), channel_id=1, source_target_pairs={{0,15},{1,0},{2,1},{3,2},{4,3},{5,4},{6,5},{7,6},{8,7},{9,8},{10,9... | collective-permute-start | bytes 3145736 | tf_op jit(solution)/shard_map/while/body/eval_jaxpr/ppermute | solution.py:17
  421.9 20.5 %copy-start.5 = (f32[2,3,2,512,128]{4,3,2,1,0:T(8,128)}, f32[2,3,2,512,128]{4,3,2,1,0:T(8,128)S(1)}, u32[]{:S(2)}) copy-start(f32[2,3,2,512,128]{4,3,2,1,0:T(8,128)S(1)} %get-tuple-element.493) | copy-start | bytes 9437188 | tf_op jit(solution)/shard_map/while
  429.0 12.5 %copy-start.3 = (f32[2,3,2,512,128]{4,3,2,1,0:T(8,128)}, f32[2,3,2,512,128]{4,3,2,1,0:T(8,128)S(1)}, u32[]{:S(2)}) copy-start(f32[2,3,2,512,128]{4,3,2,1,0:T(8,128)S(1)} %fusion.58) | copy-start | bytes 9437188 | tf_op jit(solution)/shard_map/while
  429.1 11.8 %collective-permute-start.1 = (f32[2,2,1,512,128]{4,3,2,1,0:T(8,128)S(1)}, f32[2,2,1,512,128]{4,3,2,1,0:T(8,128)S(1)}, u32[]{:S(2)}, u32[]{:S(2)}) collective-permute-start(f32[2,2,1,512,128]{4,3,2,1,0:T(8,128)S(1)} %slice.477), channel_id=1, source_target_pairs={{0,1},{1,2},{2,3},{3,4},{4,5},{5,6},{6,7},{7,8},{8,9},{9,10},{10,1... | collective-permute-start | bytes 3145736 | tf_op jit(solution)/shard_map/while/body/eval_jaxpr/ppermute | solution.py:17
  445.1 18.9 %collective-permute-start = (f32[2,2,1,512,128]{4,3,0,2,1:T(8,128)}, f32[2,2,1,512,128]{4,3,0,2,1:T(8,128)}, u32[]{:S(2)}, u32[]{:S(2)}) collective-permute-start(f32[2,2,1,512,128]{4,3,0,2,1:T(8,128)} %slice.472), channel_id=1, source_target_pairs={{0,15},{1,0},{2,1},{3,2},{4,3},{5,4},{6,5},{7,6},{8,7},{9,8},{10,9... | collective-permute-start | bytes 3145736 | tf_op jit(solution)/shard_map/while/body/eval_jaxpr/ppermute | solution.py:17
  464.0 20.5 %copy-start.5 = (f32[2,3,2,512,128]{4,3,2,1,0:T(8,128)}, f32[2,3,2,512,128]{4,3,2,1,0:T(8,128)S(1)}, u32[]{:S(2)}) copy-start(f32[2,3,2,512,128]{4,3,2,1,0:T(8,128)S(1)} %get-tuple-element.493) | copy-start | bytes 9437188 | tf_op jit(solution)/shard_map/while
  471.2 11.8 %collective-permute-start.1 = (f32[2,2,1,512,128]{4,3,2,1,0:T(8,128)S(1)}, f32[2,2,1,512,128]{4,3,2,1,0:T(8,128)S(1)}, u32[]{:S(2)}, u32[]{:S(2)}) collective-permute-start(f32[2,2,1,512,128]{4,3,2,1,0:T(8,128)S(1)} %slice.477), channel_id=1, source_target_pairs={{0,1},{1,2},{2,3},{3,4},{4,5},{5,6},{6,7},{7,8},{8,9},{9,10},{10,1... | collective-permute-start | bytes 3145736 | tf_op jit(solution)/shard_map/while/body/eval_jaxpr/ppermute | solution.py:17
  487.3 18.9 %collective-permute-start = (f32[2,2,1,512,128]{4,3,0,2,1:T(8,128)}, f32[2,2,1,512,128]{4,3,0,2,1:T(8,128)}, u32[]{:S(2)}, u32[]{:S(2)}) collective-permute-start(f32[2,2,1,512,128]{4,3,0,2,1:T(8,128)} %slice.472), channel_id=1, source_target_pairs={{0,15},{1,0},{2,1},{3,2},{4,3},{5,4},{6,5},{7,6},{8,7},{9,8},{10,9... | collective-permute-start | bytes 3145736 | tf_op jit(solution)/shard_map/while/body/eval_jaxpr/ppermute | solution.py:17
  506.1 20.5 %copy-start.5 = (f32[2,3,2,512,128]{4,3,2,1,0:T(8,128)}, f32[2,3,2,512,128]{4,3,2,1,0:T(8,128)S(1)}, u32[]{:S(2)}) copy-start(f32[2,3,2,512,128]{4,3,2,1,0:T(8,128)S(1)} %get-tuple-element.493) | copy-start | bytes 9437188 | tf_op jit(solution)/shard_map/while
  513.3 12.5 %copy-start.3 = (f32[2,3,2,512,128]{4,3,2,1,0:T(8,128)}, f32[2,3,2,512,128]{4,3,2,1,0:T(8,128)S(1)}, u32[]{:S(2)}) copy-start(f32[2,3,2,512,128]{4,3,2,1,0:T(8,128)S(1)} %fusion.58) | copy-start | bytes 9437188 | tf_op jit(solution)/shard_map/while
  513.3 11.8 %collective-permute-start.1 = (f32[2,2,1,512,128]{4,3,2,1,0:T(8,128)S(1)}, f32[2,2,1,512,128]{4,3,2,1,0:T(8,128)S(1)}, u32[]{:S(2)}, u32[]{:S(2)}) collective-permute-start(f32[2,2,1,512,128]{4,3,2,1,0:T(8,128)S(1)} %slice.477), channel_id=1, source_target_pairs={{0,1},{1,2},{2,3},{3,4},{4,5},{5,6},{6,7},{7,8},{8,9},{9,10},{10,1... | collective-permute-start | bytes 3145736 | tf_op jit(solution)/shard_map/while/body/eval_jaxpr/ppermute | solution.py:17
  (91 other events, 228.7 us)
where the time goes:
time: 538 us; the launch traced here: 530 us
  other arithmetic  194 us (36%)
  waiting for transfers between devices  138 us (26%)
  local copies, waits for them, and re-layouts  131 us (24%)
  starting transfers between devices  61.2 us (11%)
    ppermute x24, waiting for transfers between devices, shifted(): lax.ppermute(value, axis, [(i, (i + by) % size) for i in range(size)])  138 us
    add x12, other arithmetic, update_electric(): polar = polar + time_step * current  78.9 us
    ppermute x24, starting transfers between devices, shifted(): lax.ppermute(value, axis, [(i, (i + by) % size) for i in range(size)])  61.2 us
    slice x24, local copies, waits for them, and re-layouts, next_z(): return jnp.concatenate([field[..., 1:], zeros], axis=-1)  36.6 us
    sub x60, other arithmetic, cmul(): field[0] * cosv - field[1] * sinv  34.4 us
    while x228, local copies, waits for them, and re-layouts  25.7 us
    select_n x12, other arithmetic, advance(): right = jnp.where(at_last, cmul(right, cos_x, sin_x), right)  17.2 us
    add x12, other arithmetic, update_electric(): efield = efield + ce * (kurl - current)  15.6 us
  transfers between devices with their start and end apart: 24, of which 13 were waited for; matrix products, arithmetic and copies ran while one was open for 32% of the time, Pallas kernels for 0%

commit v1 on v0

v1 whole, which is shorter than its diff:
```python
import functools
import math

import jax
import jax.numpy as jnp
from jax import lax
from jax.experimental import pallas as pl
from jax.experimental.pallas import tpu as pltpu
from jax.sharding import PartitionSpec as P

ITERS = 12
KGRID = 16
CHUNKS = 8
BLOCK = 8
UNROLL = 2
PAD = 8

time_step = 0.5


def kernel(e_in, h_in, lab_in, table, phase, e_out, h_out,
           e, h, pol, cur, coef, lab, ge, gh,
           in_sem, out_sem, se_sem, re_sem, sh_sem, rh_sem):
    planes, rows, width = lab.shape
    chunk = rows // CHUNKS
    gx = lax.axis_size("gx")
    me = lax.axis_index("gx")
    right, left = lax.rem(me + 1, gx), lax.rem(me + gx - 1, gx)
    last = planes - 1

    def rows_of(c):
        return pl.ds(pl.multiple_of(c * chunk, chunk), chunk)

    def h_rows_of(c):
        return pl.ds(pl.multiple_of(c * chunk + PAD, 8), chunk)

    loads = [
        pltpu.make_async_copy(e_in, e.at[:, :, :, pl.ds(0, rows)], in_sem.at[0]),
        pltpu.make_async_copy(lab_in, lab, in_sem.at[2]),
        pltpu.make_async_copy(h_in, h.at[:, :, :, pl.ds(PAD, rows)], in_sem.at[1]),
    ]
    for load in loads:
        load.start()

    barrier = pltpu.get_barrier_semaphore()
    for other in (left, right):
        pl.semaphore_signal(barrier, inc=1, device_id={"gx": other},
                            device_id_type=pl.DeviceIdType.MESH)
    pl.semaphore_wait(barrier, 2)

    def send_e(c, source):
        return pltpu.make_async_remote_copy(
            src_ref=source.at[:, pl.ds(1, 2), 0, rows_of(c)],
            dst_ref=ge.at[:, :, rows_of(c)],
            send_sem=se_sem.at[c], recv_sem=re_sem.at[c],
            device_id={"gx": left}, device_id_type=pl.DeviceIdType.MESH)

    def send_h(c):
        return pltpu.make_async_remote_copy(
            src_ref=h.at[:, pl.ds(1, 2), last, h_rows_of(c)],
            dst_ref=gh.at[:, :, rows_of(c)],
            send_sem=sh_sem.at[c], recv_sem=rh_sem.at[c],
            device_id={"gx": right}, device_id_type=pl.DeviceIdType.MESH)

    def store_out(c):
        return pltpu.make_async_copy(e.at[:, :, :, rows_of(c)],
                                     e_out.at[:, :, :, rows_of(c)], out_sem.at[c])

    def store_h_out(c):
        return pltpu.make_async_copy(h.at[:, :, :, h_rows_of(c)],
                                     h_out.at[:, :, :, rows_of(c)], out_sem.at[CHUNKS + c])

    @pl.loop(0, CHUNKS)
    def _(c):
        send_e(c, e_in).start()

    zero = jnp.zeros((BLOCK, width), jnp.float32)

    loads[1].wait()

    @pl.loop(0, rows // BLOCK)
    def _(i):
        here = pl.ds(pl.multiple_of(i * BLOCK, BLOCK), BLOCK)
        for x in range(planes):
            label = lab[x, here]
            masks = [label == k for k in range(table.shape[1])]
            for which in range(4):
                picked = zero
                for k, mask in enumerate(masks):
                    picked = picked + jnp.where(mask, table[which, k], jnp.float32(0.0))
                coef[which, x, here] = picked
            for ri in range(2):
                for a in range(3):
                    pol[ri, a, x, here] = zero
                    cur[ri, a, x, here] = zero

    cos_r, sin_r, cos_l, sin_l, cos_y, sin_y = [phase[i] for i in range(6)]
    lane = lax.broadcasted_iota(jnp.int32, (BLOCK, width), 1)
    not_end = lane < width - 1
    not_start = lane > 0

    def wrap_e():
        for a in (0, 2):
            for x in range(planes):
                re, im = e[0, a, x, 0:1], e[1, a, x, 0:1]
                e[0, a, x, rows:rows + 1] = re * cos_y - im * sin_y
                e[1, a, x, rows:rows + 1] = re * sin_y + im * cos_y

    def wrap_h():
        end = PAD + rows - 1
        for a in (0, 2):
            for x in range(planes):
                re, im = h[0, a, x, end:end + 1], h[1, a, x, end:end + 1]
                h[0, a, x, PAD - 1:PAD] = re * cos_y + im * sin_y
                h[1, a, x, PAD - 1:PAD] = im * cos_y - re * sin_y

    def turned(re, im, cosv, sinv):
        return re * cosv - im * sinv, re * sinv + im * cosv

    def next_z(f):
        return jnp.where(not_end, pltpu.roll(f, width - 1, 1), 0.0)

    def prev_z(f):
        return jnp.where(not_start, pltpu.roll(f, 1, 1), 0.0)

    def magnetic(x, r):
        here = pl.ds(pl.multiple_of(r, BLOCK), BLOCK)
        there = pl.ds(pl.multiple_of(r + PAD, 8), BLOCK)
        up = pl.ds(r + 1, BLOCK)
        if x == last:
            beyond = [turned(ge[0, a, here], ge[1, a, here], cos_r, sin_r) for a in range(2)]
        else:
            beyond = [(e[0, a, x + 1, here], e[1, a, x + 1, here]) for a in (1, 2)]
        for ri in range(2):
            ex, ey, ez = [e[ri, a, x, here] for a in range(3)]
            cx = (e[ri, 2, x, up] - ez) - (next_z(ey) - ey)
            cy = (next_z(ex) - ex) - (beyond[1][ri] - ez)
            cz = (beyond[0][ri] - ey) - (e[ri, 0, x, up] - ex)
            for a, curl in enumerate((cx, cy, cz)):
                h[ri, a, x, there] = h[ri, a, x, there] - time_step * curl

    def electric(x, r):
        here = pl.ds(pl.multiple_of(r, BLOCK), BLOCK)
        there = pl.ds(pl.multiple_of(r + PAD, 8), BLOCK)
        down = pl.ds(r + PAD - 1, BLOCK)
        ce, ja, jb, de = [coef[k, x, here] for k in range(4)]
        if x == 0:
            before = [turned(gh[0, a, here], gh[1, a, here], cos_l, sin_l) for a in range(2)]
        else:
            before = [(h[0, a, x - 1, there], h[1, a, x - 1, there]) for a in (1, 2)]
        for ri in range(2):
            hx, hy, hz = [h[ri, a, x, there] for a in range(3)]
            kx = (hz - h[ri, 2, x, down]) - (hy - prev_z(hy))
            ky = (hx - prev_z(hx)) - (hz - before[1][ri])
            kz = (hy - before[0][ri]) - (hx - h[ri, 0, x, down])
            for a, kurl in enumerate((kx, ky, kz)):
                field, polar = e[ri, a, x, here], pol[ri, a, x, here]
                current = ja * cur[ri, a, x, here] + jb * (de * field - polar)
                cur[ri, a, x, here] = current
                pol[ri, a, x, here] = polar + time_step * current
                e[ri, a, x, here] = field + ce * (kurl - current)

    def sweep(update, order, c):
        def one(i, carry):
            for x in order:
                update(x, c * chunk + i * BLOCK)
            return carry
        lax.fori_loop(0, chunk // BLOCK, one, 0, unroll=UNROLL)

    loads[0].wait()
    loads[2].wait()
    wrap_e()

    @pl.loop(0, ITERS)
    def _(step):
        @pl.loop(0, CHUNKS)
        def _(c):
            @pl.when(step > 0)
            def _():
                send_h(c).wait_send()
            send_e(c, e).wait_recv()
            sweep(magnetic, range(planes - 1, -1, -1), c)
            send_h(c).start()

        wrap_h()

        @pl.when(step == ITERS - 1)
        def _():
            @pl.loop(0, CHUNKS)
            def _(c):
                store_h_out(c).start()

        @pl.loop(0, CHUNKS)
        def _(c):
            send_e(c, e).wait_send()
            send_h(c).wait_recv()
            sweep(electric, range(planes), c)

            @pl.when(step < ITERS - 1)
            def _():
                send_e(c, e).start()

            @pl.when(step == ITERS - 1)
            def _():
                store_out(c).start()

        wrap_e()

    @pl.loop(0, CHUNKS)
    def _(c):
        send_h(c).wait_send()
        store_h_out(c).wait()
        store_out(c).wait()


def shards(e_field, h_field, labels, kpoint, eps_inf, delta_eps, omega_zero, damping):
    theta_x = jnp.float32(2.0 * math.pi) * kpoint[0].astype(jnp.float32) / KGRID
    theta_y = jnp.float32(2.0 * math.pi) * kpoint[1].astype(jnp.float32) / KGRID
    cos_x, sin_x = (jnp.cos(theta_x), jnp.sin(theta_x))
    cos_y, sin_y = (jnp.cos(theta_y), jnp.sin(theta_y))
    half = damping * time_step / 2.0
    table = jnp.stack([
        time_step / eps_inf,
        (1.0 - half) / (1.0 + half),
        time_step * omega_zero * omega_zero / (1.0 + half),
        delta_eps,
    ])
    position = lax.axis_index("gx")
    at_first = position == 0
    at_last = position == lax.axis_size("gx") - 1
    one, nought = jnp.float32(1.0), jnp.float32(0.0)
    phase = jnp.stack([
        jnp.where(at_last, cos_x, one), jnp.where(at_last, sin_x, nought),
        jnp.where(at_first, cos_x, one), jnp.where(at_first, -sin_x, nought),
        cos_y, sin_y,
    ])
    planes, rows, width = labels.shape
    state = (2, 3, planes, rows, width)
    padded = (2, 3, planes, rows + PAD, width)
    anywhere = pl.BlockSpec(memory_space=pl.ANY)
    scalars = pl.BlockSpec(memory_space=pltpu.SMEM)
    return pl.pallas_call(
        kernel,
        out_shape=(jax.ShapeDtypeStruct(state, jnp.float32),) * 2,
        in_specs=[anywhere] * 3 + [scalars] * 2,
        out_specs=(anywhere, anywhere),
        scratch_shapes=[
            pltpu.VMEM(padded, jnp.float32),
            pltpu.VMEM(padded, jnp.float32),
            pltpu.VMEM(state, jnp.float32),
            pltpu.VMEM(state, jnp.float32),
            pltpu.VMEM((4, planes, rows, width), jnp.float32),
            pltpu.VMEM((planes, rows, width), jnp.int32),
            pltpu.VMEM((2, 2, rows, width), jnp.float32),
            pltpu.VMEM((2, 2, rows, width), jnp.float32),
            pltpu.SemaphoreType.DMA((3,)),
            pltpu.SemaphoreType.DMA((2 * CHUNKS,)),
            pltpu.SemaphoreType.DMA((CHUNKS,)),
            pltpu.SemaphoreType.DMA((CHUNKS,)),
            pltpu.SemaphoreType.DMA((CHUNKS,)),
            pltpu.SemaphoreType.DMA((CHUNKS,)),
        ],
        compiler_params=pltpu.CompilerParams(collective_id=0, has_side_effects=True),
    )(e_field, h_field, labels, table, phase)


def solution(mesh):
    placed = (
        P(None, None, ("kpt", "gx"), None, None),
        P(None, None, ("kpt", "gx"), None, None),
        P(("kpt", "gx"), None, None),
        P("kpt"),
        P(),
        P(),
        P(),
        P(),
    )
    return jax.shard_map(
        shards,
        mesh=mesh,
        in_specs=placed,
        out_specs=(
            P(None, None, ("kpt", "gx"), None, None),
            P(None, None, ("kpt", "gx"), None, None),
        ),
        check_vma=False,
    )
```

time: 538 us -> 337 us (0.63)
  the two profiles are of different devices: /device:TPU:1 before, /device:TPU:12 now
where the time goes in v1:
time: 337 us
  Pallas kernels  325 us (96%)
  local copies, waits for them, and re-layouts  7.48 us (2%)
    pallas_call x1, Pallas kernels, shards(): pl.pallas_call(kernel, out_shape=(jax.ShapeDtypeStruct(state, jnp.float32...  325 us

profile of v1, /device:TPU:12, one launch (start us, length us, event | category | flops | bytes accessed | tf_op | source)
XLA Modules:
  0.0 336.9 jit_solution(9836426030335392182)
XLA Ops:
  0.6 1.3 fusion.3
  3.6 0.6 stack.41.phase
  4.2 0.7 fusion.1
  4.9 1.2 pad_maximum_fusion.table
  6.1 325.2 %shard_map.95 = (f32[2,3,2,512,128]{4,3,2,1,0:T(8,128)}, f32[2,3,2,512,128]{4,3,2,1,0:T(8,128)}) custom-call(f32[2,3,2,512,128]{4,3,2,1,0:T(8,128)} %e_in.1, f32[2,3,2,512,128]{4,3,2,1,0:T(8,128)} %h_in.1, s32[2,512,128]{2,1,0:T(8,128)} %lab_in.1, f32[4,4]{1,0:T(4,128)} %pad_maximum_fusion.table, f32[6]{0:T(128)} %stack.41.phase), custom_call_target="tpu_custom_call" | custom-call | tf_op jit(solution)/shard_map/pallas_call | solution.py:242
  331.3 0.0 copy-start
  331.3 3.9 %copy.12 = f32[2,3,2,512,128]{4,3,2,1,0:T(8,128)} copy(f32[2,3,2,512,128]{4,3,2,1,0:T(8,128)} %get-tuple-element.9) | data formatting | bytes 6291456
  335.2 0.0 copy-done
  335.2 1.7 copy.13
Async XLA Ops:
  331.3 3.9 %copy-start = (f32[2,3,2,512,128]{4,3,2,1,0:T(8,128)S(1)}, f32[2,3,2,512,128]{4,3,2,1,0:T(8,128)}, u32[]{:S(2)}) copy-start(f32[2,3,2,512,128]{4,3,2,1,0:T(8,128)} %get-tuple-element.10) | copy-start | bytes 9437188

commit v2 on v0

v2 whole, which is shorter than its diff:
```python
import functools
import math

import jax
import jax.numpy as jnp
from jax import lax
from jax.experimental import pallas as pl
from jax.experimental.pallas import tpu as pltpu
from jax.sharding import PartitionSpec as P

ITERS = 12
KGRID = 16
CHUNKS = 4
BLOCK = 8
UNROLL = 2
PAD = 8

time_step = 0.5


class Tile:
    def __init__(self, refs, sems, left, right, turns):
        self.e, self.h, self.pol, self.cur, self.coef, self.lab, self.ge, self.gh = refs[:8]
        self.e_stage, self.h_stage, self.e_edge, self.h_edge = refs[8:]
        self.se, self.re, self.sh, self.rh = sems
        self.left, self.right = left, right
        self.turn_r, self.turn_l, self.turn_up, self.turn_down = turns
        self.planes, self.rows, self.width = self.lab.shape
        self.chunk = self.rows // CHUNKS

    def send_e(self, c):
        here = pl.ds(c * self.chunk, self.chunk)
        return pltpu.make_async_remote_copy(
            src_ref=self.e.at[:, pl.ds(1, 2), 0, here], dst_ref=self.ge.at[:, :, here],
            send_sem=self.se.at[c], recv_sem=self.re.at[c],
            device_id={"gx": self.left}, device_id_type=pl.DeviceIdType.MESH)

    def send_h(self, c):
        here, there = pl.ds(c * self.chunk, self.chunk), pl.ds(c * self.chunk + PAD, self.chunk)
        return pltpu.make_async_remote_copy(
            src_ref=self.h.at[:, pl.ds(1, 2), self.planes - 1, there], dst_ref=self.gh.at[:, :, here],
            send_sem=self.sh.at[c], recv_sem=self.rh.at[c],
            device_id={"gx": self.right}, device_id_type=pl.DeviceIdType.MESH)

    def clear(self, table):
        zero = jnp.zeros((BLOCK, self.width), jnp.float32)

        @pl.loop(0, self.rows // BLOCK)
        def _(i):
            here = pl.ds(pl.multiple_of(i * BLOCK, BLOCK), BLOCK)
            for x in range(self.planes):
                label = self.lab[x, here]
                masks = [label == k for k in range(table.shape[1])]
                for which in range(4):
                    picked = zero
                    for k, mask in enumerate(masks):
                        picked = picked + jnp.where(mask, table[which, k], jnp.float32(0.0))
                    self.coef[which, x, here] = picked
                for ri in range(2):
                    for a in range(3):
                        self.pol[ri, a, x, here] = zero
                        self.cur[ri, a, x, here] = zero

    def stage_e(self):
        for x in range(self.planes):
            for ri in range(2):
                for j, a in enumerate((0, 2)):
                    row = 2 * ri + j
                    self.e_stage[x, row:row + 1] = self.e[ri, a, x, 0:1]

    def stage_h(self):
        end = PAD + self.rows - 1
        for x in range(self.planes):
            for ri in range(2):
                for j, a in enumerate((0, 2)):
                    row = 2 * ri + j
                    self.h_stage[x, row:row + 1] = self.h[ri, a, x, end:end + 1]

    def take_edge(self, edge, field, at, turn):
        for x in range(self.planes):
            for j, a in enumerate((0, 2)):
                re, im = turned(edge[x, j:j + 1], edge[x, 2 + j:3 + j], *turn)
                field[0, a, x, at:at + 1] = re
                field[1, a, x, at:at + 1] = im

    def take_e(self):
        self.take_edge(self.e_edge, self.e, self.rows, self.turn_up)

    def take_h(self):
        self.take_edge(self.h_edge, self.h, PAD - 1, self.turn_down)

    def magnetic(self, x, r, next_z, prev_z):
        e, h, ge = self.e, self.h, self.ge
        here = pl.ds(pl.multiple_of(r, BLOCK), BLOCK)
        there = pl.ds(pl.multiple_of(r + PAD, 8), BLOCK)
        up = pl.ds(r + 1, BLOCK)
        if x == self.planes - 1:
            beyond = [turned(ge[0, a, here], ge[1, a, here], *self.turn_r) for a in range(2)]
        else:
            beyond = [(e[0, a, x + 1, here], e[1, a, x + 1, here]) for a in (1, 2)]
        for ri in range(2):
            ex, ey, ez = [e[ri, a, x, here] for a in range(3)]
            cx = (e[ri, 2, x, up] - ez) - (next_z(ey) - ey)
            cy = (next_z(ex) - ex) - (beyond[1][ri] - ez)
            cz = (beyond[0][ri] - ey) - (e[ri, 0, x, up] - ex)
            for a, curl in enumerate((cx, cy, cz)):
                h[ri, a, x, there] = h[ri, a, x, there] - time_step * curl

    def electric(self, x, r, next_z, prev_z):
        e, h, gh, pol, cur = self.e, self.h, self.gh, self.pol, self.cur
        here = pl.ds(pl.multiple_of(r, BLOCK), BLOCK)
        there = pl.ds(pl.multiple_of(r + PAD, 8), BLOCK)
        down = pl.ds(r + PAD - 1, BLOCK)
        ce, ja, jb, de = [self.coef[k, x, here] for k in range(4)]
        if x == 0:
            before = [turned(gh[0, a, here], gh[1, a, here], *self.turn_l) for a in range(2)]
        else:
            before = [(h[0, a, x - 1, there], h[1, a, x - 1, there]) for a in (1, 2)]
        for ri in range(2):
            hx, hy, hz = [h[ri, a, x, there] for a in range(3)]
            kx = (hz - h[ri, 2, x, down]) - (hy - prev_z(hy))
            ky = (hx - prev_z(hx)) - (hz - before[1][ri])
            kz = (hy - before[0][ri]) - (hx - h[ri, 0, x, down])
            for a, kurl in enumerate((kx, ky, kz)):
                field, polar = e[ri, a, x, here], pol[ri, a, x, here]
                current = ja * cur[ri, a, x, here] + jb * (de * field - polar)
                cur[ri, a, x, here] = current
                pol[ri, a, x, here] = polar + time_step * current
                e[ri, a, x, here] = field + ce * (kurl - current)

    def sweep(self, update, order, c, shifts):
        def one(i, carry):
            for x in order:
                update(x, c * self.chunk + i * BLOCK, *shifts)
            return carry
        lax.fori_loop(0, self.chunk // BLOCK, one, 0, unroll=UNROLL)


def turned(re, im, cosv, sinv):
    return re * cosv - im * sinv, re * sinv + im * cosv


def kernel(e_in, h_in, lab_in, table, phase, e_out, h_out, *scratch):
    gx = lax.axis_size("gx")
    me = lax.axis_index("gx")
    q = lax.rem(me, 4)
    base = me - q
    y = lax.div(q, 2)
    core = lax.rem(q, 2)
    local = lab_in.shape[0]
    own_refs, moved_refs = scratch[:12], scratch[12:24]
    own_sems, moved_sems = scratch[24:28], scratch[28:32]
    in_sem, out_sem, sl, rl, so, ro, ees, eer, hhs, hhr = scratch[32:]
    ph = [phase[i] for i in range(12)]
    one, nought = jnp.float32(1.0), jnp.float32(0.0)
    cos_y, sin_y = ph[8], ph[9]
    own = Tile(own_refs, own_sems, lax.rem(me + gx - 1, gx), lax.rem(me + 1, gx),
               ((ph[0], ph[1]), (ph[2], ph[3]), (one, nought), (cos_y, -sin_y)))
    moved = Tile(moved_refs, moved_sems,
                 lax.rem(me + gx - 3 + 2 * core, gx), lax.rem(me + 3 - 2 * (1 - core), gx),
                 ((ph[4], ph[5]), (ph[6], ph[7]), (ph[10], ph[11]), (one, nought)))
    tiles = (own, moved)
    keep, part, width = own.rows, moved.rows, own.width

    def remote(src, dst, send, recv, to):
        return pltpu.make_async_remote_copy(
            src_ref=src, dst_ref=dst, send_sem=send, recv_sem=recv,
            device_id={"gx": to}, device_id_type=pl.DeviceIdType.MESH)

    loads = [
        pltpu.make_async_copy(lab_in.at[:, pl.ds(0, keep)], own.lab, in_sem.at[0]),
        pltpu.make_async_copy(e_in.at[:, :, :, pl.ds(0, keep)], own.e.at[:, :, :, pl.ds(0, keep)], in_sem.at[1]),
        pltpu.make_async_copy(h_in.at[:, :, :, pl.ds(0, keep)], own.h.at[:, :, :, pl.ds(PAD, keep)], in_sem.at[2]),
    ]
    for load in loads:
        load.start()

    barrier = pltpu.get_barrier_semaphore()
    others = [base + lax.rem(q + k, 4) for k in (1, 2, 3)]
    others += [lax.rem(me + gx + k, gx) for k in (-3, -1, 1, 3)]
    for other in others:
        pl.semaphore_signal(barrier, inc=1, device_id={"gx": other},
                            device_id_type=pl.DeviceIdType.MESH)
    pl.semaphore_wait(barrier, len(others))

    def move_in(half, slot):
        rows = pl.ds(keep + half * part, part)
        planes = pl.ds(slot * local, local)
        return ((e_in.at[:, :, :, rows], moved.e.at[:, :, planes, pl.ds(0, part)]),
                (lab_in.at[:, rows], moved.lab.at[planes]),
                (h_in.at[:, :, :, rows], moved.h.at[:, :, planes, pl.ds(PAD, part)]))

    def each_move_in(act):
        for half in range(2):
            self_q = 3 * half
            for k, (src, dst) in enumerate(move_in(half, self_q % 2)):
                @pl.when(q == self_q)
                def _():
                    act(None, pltpu.make_async_copy(src, dst, rl.at[k, self_q % 2]))
            for slot in range(2):
                for k, (src, dst) in enumerate(move_in(half, slot)):
                    @pl.when((q != self_q) & (core == slot))
                    def _():
                        act(remote(src, dst, sl.at[k, half], rl.at[k, slot], base + 2 * half + y), None)

    each_move_in(lambda far, near: (far or near).start())

    def wait_in(k):
        for slot in range(2):
            src, dst = move_in(0, slot)[k]
            remote(src, dst, sl.at[k, 0], rl.at[k, slot], base + lax.rem(q + 1, 4)).wait_recv()

    def edges(f, o_stage, a_stage, o_edge, a_edge, ss, rs, act):
        for slot in range(2):
            src, dst = o_stage, a_edge.at[pl.ds(slot * local, local)]

            @pl.when((core == slot) & (q != 3 * f))
            def _():
                act(remote(src, dst, ss.at[0], rs.at[1 + slot], base + 2 * f + y), None)
        @pl.when(q == 3 * f)
        def _():
            act(None, pltpu.make_async_copy(o_stage, a_edge.at[pl.ds(f * local, local)], rs.at[1 + f]))
        for i in range(2):
            src, dst = a_stage.at[pl.ds(i * local, local)], o_edge
            if i == 1 - f:
                here = (y == 1 - f) & (core == 1 - f)
                away = (y == 1 - f) & (core != 1 - f)

                @pl.when(here)
                def _():
                    act(None, pltpu.make_async_copy(src, dst, rs.at[0]))
            else:
                away = y == 1 - f

            @pl.when(away)
            def _():
                act(remote(src, dst, ss.at[1 + i], rs.at[0], base + 2 * core + i), None)

        @pl.when(y == f)
        def _():
            act(remote(a_stage, a_edge, ss.at[3], rs.at[1], base + 2 * (1 - f) + core), None)

    def edges_arrive(f, o_stage, a_stage, o_edge, a_edge, ss, rs):
        to = base + lax.rem(q + 1, 4)
        remote(o_stage, o_edge, ss.at[0], rs.at[0], to).wait_recv()

        @pl.when(y == f)
        def _():
            for slot in range(2):
                remote(o_stage, a_edge.at[pl.ds(slot * local, local)], ss.at[0], rs.at[1 + slot], to).wait_recv()

        @pl.when(y != f)
        def _():
            remote(a_stage, a_edge, ss.at[3], rs.at[1], to).wait_recv()

    e_edges = (1, own.e_stage, moved.e_stage, own.e_edge, moved.e_edge, ees, eer)
    h_edges = (0, own.h_stage, moved.h_stage, own.h_edge, moved.h_edge, hhs, hhr)

    def start(far, near):
        (far or near).start()

    def sent(far, near):
        if far is not None:
            far.wait_send()

    lane = lax.broadcasted_iota(jnp.int32, (BLOCK, width), 1)
    not_end = lane < width - 1
    not_start = lane > 0

    def next_z(f):
        return jnp.where(not_end, pltpu.roll(f, width - 1, 1), 0.0)

    def prev_z(f):
        return jnp.where(not_start, pltpu.roll(f, 1, 1), 0.0)

    shifts = (next_z, prev_z)
    sequence = [c ^ 1 for c in range(CHUNKS)]

    loads[0].wait()
    own.clear(table)
    loads[1].wait()
    for c in sequence:
        own.send_e(c).start()
    wait_in(0)
    for c in sequence:
        moved.send_e(c).start()
    own.stage_e()
    moved.stage_e()
    wait_in(1)
    moved.clear(table)
    edges(*e_edges, start)
    loads[2].wait()
    wait_in(2)

    def store(k, ref, out):
        rows = pl.ds(0, keep)
        skip = pl.ds(PAD if k else 0, keep)
        return pltpu.make_async_copy(ref.at[:, :, :, skip], out.at[:, :, :, rows], out_sem.at[k])

    def each_move_out(k, ref, out, act):
        for half in range(2):
            rows = pl.ds(keep + half * part, part)
            for i in range(2):
                src = ref.at[:, :, pl.ds(i * local, local), pl.ds(PAD if k else 0, part)]
                dst = out.at[:, :, :, rows]
                away = y == half
                if i == half:
                    @pl.when((y == half) & (core == half))
                    def _():
                        act(None, pltpu.make_async_copy(src, dst, ro.at[k, half]))
                    away = away & (core != half)

                @pl.when(away)
                def _():
                    act(remote(src, dst, so.at[k, i], ro.at[k, half], base + 2 * core + i), None)

    def wait_out(k, ref, out):
        for half in range(2):
            src = ref.at[:, :, pl.ds(0, local), pl.ds(PAD if k else 0, part)]
            dst = out.at[:, :, :, pl.ds(keep + half * part, part)]
            remote(src, dst, so.at[k, 0], ro.at[k, half], base + lax.rem(q + 1, 4)).wait_recv()

    @pl.loop(0, ITERS)
    def _(step):
        for c in sequence:
            if c == CHUNKS - 1:
                edges_arrive(*e_edges)
                for tile in tiles:
                    tile.take_e()
            for tile in tiles:
                @pl.when(step > 0)
                def _():
                    tile.send_h(c).wait_send()
                tile.send_e(c).wait_recv()
                tile.sweep(tile.magnetic, range(tile.planes - 1, -1, -1), c, shifts)
                tile.send_h(c).start()
            if c == CHUNKS - 1:
                @pl.when(step > 0)
                def _():
                    edges(*h_edges, sent)
                for tile in tiles:
                    tile.stage_h()
                edges(*h_edges, start)

        @pl.when(step == ITERS - 1)
        def _():
            store(1, own.h, h_out).start()
            each_move_out(1, moved.h, h_out, start)

        for c in sequence:
            if c == 0:
                edges_arrive(*h_edges)
                for tile in tiles:
                    tile.take_h()
            for tile in tiles:
                tile.send_e(c).wait_send()
                tile.send_h(c).wait_recv()
                tile.sweep(tile.electric, range(tile.planes), c, shifts)

                @pl.when(step < ITERS - 1)
                def _():
                    tile.send_e(c).start()
            if c == 0:
                edges(*e_edges, sent)

                @pl.when(step < ITERS - 1)
                def _():
                    for tile in tiles:
                        tile.stage_e()
                    edges(*e_edges, start)

    store(0, own.e, e_out).start()
    each_move_out(0, moved.e, e_out, start)
    each_move_in(sent)
    edges(*h_edges, sent)
    for c in range(CHUNKS):
        for tile in tiles:
            tile.send_h(c).wait_send()
    for k, ref, mref, out in ((0, own.e, moved.e, e_out), (1, own.h, moved.h, h_out)):
        store(k, ref, out).wait()
        each_move_out(k, mref, out, sent)
        wait_out(k, mref, out)


def shards(e_field, h_field, labels, kpoint, eps_inf, delta_eps, omega_zero, damping):
    theta_x = jnp.float32(2.0 * math.pi) * kpoint[0].astype(jnp.float32) / KGRID
    theta_y = jnp.float32(2.0 * math.pi) * kpoint[1].astype(jnp.float32) / KGRID
    cos_x, sin_x = (jnp.cos(theta_x), jnp.sin(theta_x))
    cos_y, sin_y = (jnp.cos(theta_y), jnp.sin(theta_y))
    half = damping * time_step / 2.0
    table = jnp.stack([
        time_step / eps_inf,
        (1.0 - half) / (1.0 + half),
        time_step * omega_zero * omega_zero / (1.0 + half),
        delta_eps,
    ])
    position = lax.axis_index("gx")
    at_first = position == 0
    at_last = position == lax.axis_size("gx") - 1
    one, nought = jnp.float32(1.0), jnp.float32(0.0)
    size = lax.axis_size("gx")
    y = lax.rem(lax.div(position, 2), 2)
    moved_first = (position < 4) & (lax.rem(position, 2) == 0)
    moved_last = (position >= size - 4) & (lax.rem(position, 2) == 1)

    def turn(where, cosv, sinv):
        return [jnp.where(where, cosv, one), jnp.where(where, sinv, nought)]

    phase = jnp.stack(
        turn(at_last, cos_x, sin_x) + turn(at_first, cos_x, -sin_x)
        + turn(moved_last, cos_x, sin_x) + turn(moved_first, cos_x, -sin_x)
        + [cos_y, sin_y] + turn(y == 1, cos_y, sin_y))
    planes, rows, width = labels.shape
    state = (2, 3, planes, rows, width)

    def tile_scratch(planes, rows):
        field = (2, 3, planes, rows, width)
        padded = (2, 3, planes, rows + PAD, width)
        return ([pltpu.VMEM(shape, jnp.float32) for shape in (padded, padded, field, field, (4, planes, rows, width))]
                + [pltpu.VMEM((planes, rows, width), jnp.int32)]
                + [pltpu.VMEM((2, 2, rows, width), jnp.float32)] * 2
                + [pltpu.VMEM((planes, 8, width), jnp.float32)] * 4)

    dma = pltpu.SemaphoreType.DMA
    anywhere = pl.BlockSpec(memory_space=pl.ANY)
    scalars = pl.BlockSpec(memory_space=pltpu.SMEM)
    return pl.pallas_call(
        kernel,
        out_shape=(jax.ShapeDtypeStruct(state, jnp.float32),) * 2,
        in_specs=[anywhere] * 3 + [scalars] * 2,
        out_specs=(anywhere, anywhere),
        scratch_shapes=tile_scratch(planes, rows // 2) + tile_scratch(2 * planes, rows // 4)
        + [dma((CHUNKS,))] * 8
        + [dma((3,)), dma((2,)), dma((3, 2)), dma((3, 2)), dma((2, 2)), dma((2, 2))]
        + [dma((4,)), dma((3,)), dma((4,)), dma((3,))],
        compiler_params=pltpu.CompilerParams(collective_id=0, has_side_effects=True),
    )(e_field, h_field, labels, table, phase)


def solution(mesh):
    placed = (
        P(None, None, ("kpt", "gx"), None, None),
        P(None, None, ("kpt", "gx"), None, None),
        P(("kpt", "gx"), None, None),
        P("kpt"),
        P(),
        P(),
        P(),
        P(),
    )
    return jax.shard_map(
        shards,
        mesh=mesh,
        in_specs=placed,
        out_specs=(
            P(None, None, ("kpt", "gx"), None, None),
            P(None, None, ("kpt", "gx"), None, None),
        ),
        check_vma=False,
    )
```

time: 538 us -> 244 us (0.45); the launches traced: 530 us -> 244 us
  Pallas kernels: 0 us -> 232 us
  other arithmetic: 194 us -> 1.94 us
  waiting for transfers between devices: 138 us -> 0 us
  local copies, waits for them, and re-layouts: 131 us -> 7.49 us
  starting transfers between devices: 61.2 us -> 0 us
    pallas_call x0 -> x1, Pallas kernels: none -> 232 us  [shards(): pl.pallas_call(kernel, out_shape=(jax.ShapeDtypeStruct(state, jnp.float32...]
    ppermute x24 -> x0, waiting for transfers between devices: 138 us -> none  [shifted(): lax.ppermute(value, axis, [(i, (i + by) % size) for i in range(size)])]
    add x26 -> x0, other arithmetic: 109 us -> none  [the longest x12 78.9 us: update_electric(): polar = polar + time_step * current]
    ppermute x24 -> x0, starting transfers between devices: 61.2 us -> none  [shifted(): lax.ppermute(value, axis, [(i, (i + by) % size) for i in range(size)])]
    slice x88 -> x1, local copies, waits for them, and re-layouts: 54.2 us -> 1.31 us  [shards(): theta_y = jnp.float32(2.0 * math.pi) * kpoint[1].astype(jnp.float32) / KGRID]
    sub x84 -> x0, other arithmetic: 45.6 us -> none  [the longest x60 34.4 us: cmul(): field[0] * cosv - field[1] * sinv]
    concatenate x48 -> x0, local copies, waits for them, and re-layouts: 26.6 us -> none  [the longest x12 15.5 us: next_y(): return jnp.concatenate([rolled[..., :-1, :], last], axis=-2)]
    while x228 -> x0, local copies, waits for them, and re-layouts: 25.7 us -> none
  transfers between devices with their start and end apart: 24 -> 0, of which waited for: 13 -> 0; matrix products, arithmetic and copies ran while one was open for 32% -> 0% of each run, Pallas kernels for 0% -> 0%
where the time goes in v2:
time: 244 us
  Pallas kernels  232 us (95%)
  local copies, waits for them, and re-layouts  7.49 us (3%)
    pallas_call x1, Pallas kernels, shards(): pl.pallas_call(kernel, out_shape=(jax.ShapeDtypeStruct(state, jnp.float32...  232 us
    unnamed x4, local copies, waits for them, and re-layouts  5.57 us

profile of v2, /device:TPU:1, one launch (start us, length us, event | category | flops | bytes accessed | tf_op | source)
XLA Modules:
  0.0 243.6 jit_solution(15199335872050703310)
XLA Ops:
  0.7 1.3 fusion.3
  3.6 0.6 stack.65.phase
  4.2 0.7 fusion.1
  4.9 1.2 pad_maximum_fusion.table
  6.2 231.9 %shard_map.95 = (f32[2,3,2,512,128]{4,3,2,1,0:T(8,128)}, f32[2,3,2,512,128]{4,3,2,1,0:T(8,128)}) custom-call(f32[2,3,2,512,128]{4,3,2,1,0:T(8,128)} %e_in.1, f32[2,3,2,512,128]{4,3,2,1,0:T(8,128)} %h_in.1, s32[2,512,128]{2,1,0:T(8,128)} %lab_in.1, f32[4,4]{1,0:T(4,128)} %pad_maximum_fusion.table, f32[12]{0:T(128)} %stack.65.phase), custom_call_target="tpu_custom_call" | custom-call | tf_op jit(solution)/shard_map/pallas_call | solution.py:427
  238.0 0.0 copy-start
  238.1 3.9 %copy.12 = f32[2,3,2,512,128]{4,3,2,1,0:T(8,128)} copy(f32[2,3,2,512,128]{4,3,2,1,0:T(8,128)} %get-tuple-element.9) | data formatting | bytes 6291456
  242.0 0.0 copy-done
  242.0 1.7 copy.13
Async XLA Ops:
  238.0 3.9 %copy-start = (f32[2,3,2,512,128]{4,3,2,1,0:T(8,128)S(1)}, f32[2,3,2,512,128]{4,3,2,1,0:T(8,128)}, u32[]{:S(2)}) copy-start(f32[2,3,2,512,128]{4,3,2,1,0:T(8,128)} %get-tuple-element.10) | copy-start | bytes 9437188
